TPU v7x, 32 devices: a whole 2x2x4 slice. The times are simulated.
32 devices in a mesh: row: 4 (over z), col: 8 (over y, x, core).
Axes of the slice: x: 2, y: 2, z: 4, core: 2. Of those that a mesh axis runs over, the one named last changes fastest.
Arguments:
- rho_real: float32 [4096, 4096], P('row', 'col'), may hold values from -2.5 to 4, as said below
- rho_imag: float32 [4096, 4096], P('row', 'col'), may hold values from -2.5 to 2.5, as said below
- hamiltonian: bfloat16 [4096, 4096], P('row', 'col'), may hold values from -1 to 1
- amplitudes: float32 [8, 4096], replicated, may hold values from 0.15 to 0.6
- offsets: int32 [8], replicated, may hold values from -16 to 16
- active_jumps: int32 [1], replicated, may hold values from 4 to 8
Outputs:
- rho_next_real: float32 [4096, 4096], P('row', 'col')
- rho_next_imag: float32 [4096, 4096], P('row', 'col')
Inputs may be any that keep to these rules, and one draw needn't show every extreme that they name: `rho_real`: symmetric, with every diagonal entry 0.5 or more. `rho_imag`: antisymmetric.
All inputs are finite; a program needn't handle non-finite values.
Results may differ from a plain program's by a relative error of at most 0.001.
Values may be sent and summed in bfloat16 or wider, within the bound.
A program may use at most 192 MiB of HBM per device.

v0:
```python
import jax
import jax.numpy as jnp
from jax import lax
from jax.sharding import PartitionSpec as P

OMAX = 16


step_size = 0.25


def extended(cells, sides, width):
    for axis, dim in sides:
        count = lax.axis_size(axis)
        ends = count - 1
        head = lax.slice_in_dim(cells, 0, width, axis=dim)
        tail = lax.slice_in_dim(cells, cells.shape[dim] - width, cells.shape[dim], axis=dim)
        cells = jnp.concatenate(
            [
                lax.ppermute(tail, axis, [(i, (i + 1) % count) for i in range(ends)]),
                cells,
                lax.ppermute(head, axis, [((i + 1) % count, i) for i in range(ends)]),
            ],
            axis=dim,
        )
    return cells


def dissipate(matrix, padded, amplitudes, offsets, active, row_first, col_first):
    height = matrix.shape[1]
    breadth = matrix.shape[2]
    levels = amplitudes.shape[1]
    margin = (padded.shape[1] - height) // 2
    positions = jnp.arange(levels, dtype=jnp.int32)
    summed = jnp.zeros(matrix.shape, matrix.dtype)
    for jump_slot in range(amplitudes.shape[0]):
        offset = offsets[jump_slot]
        inside = (positions + offset >= 0) & (positions + offset < levels)
        strength = jnp.where(inside, amplitudes[jump_slot], 0.0)
        outflow = jnp.pad(strength * strength, (margin, margin))
        outflow = lax.dynamic_slice_in_dim(outflow, margin - offset, levels)
        row_strength = lax.dynamic_slice_in_dim(strength, row_first, height)
        col_strength = lax.dynamic_slice_in_dim(strength, col_first, breadth)
        row_outflow = lax.dynamic_slice_in_dim(outflow, row_first, height)
        col_outflow = lax.dynamic_slice_in_dim(outflow, col_first, breadth)
        corner = margin + offset
        shifted = lax.dynamic_slice(padded, (jnp.int32(0), corner, corner), (2, height, breadth))
        contribution = (
            row_strength[:, None] * col_strength[None, :] * shifted
            - 0.5 * (row_outflow[:, None] + col_outflow[None, :]) * matrix
        )
        summed = summed + jnp.where(jump_slot < active, contribution, 0.0)
    return summed


def diagonal_sum(matrix, row_first, col_first):
    row_index = lax.broadcasted_iota(jnp.int32, matrix.shape, 0) + row_first
    col_index = lax.broadcasted_iota(jnp.int32, matrix.shape, 1) + col_first
    return jnp.sum(jnp.where(row_index == col_index, matrix, 0.0))


def local(rho_real, rho_imag, hamiltonian, amplitudes, offsets, active_jumps):
    height, breadth = rho_real.shape
    levels = amplitudes.shape[1]
    row_first = lax.axis_index("row") * height
    col_first = lax.axis_index("col") * breadth
    active = active_jumps[0]
    ham_columns = lax.all_gather(hamiltonian, "row", axis=0, tiled=True)
    start_trace = lax.psum(diagonal_sum(rho_real, row_first, col_first), ("row", "col"))

    def drift(real_part, imag_part):
        real_low = real_part.astype(jnp.bfloat16)
        imag_low = imag_part.astype(jnp.bfloat16)
        row_panel = lax.all_gather(hamiltonian, "col", axis=1, tiled=True)
        pieces = (
            lax.all_gather(real_low, "row", axis=0, tiled=True),
            lax.all_gather(imag_low, "row", axis=0, tiled=True),
        )
        strip = row_panel
        left_real = jnp.dot(strip, pieces[0], preferred_element_type=jnp.float32)
        left_imag = jnp.dot(strip, pieces[1], preferred_element_type=jnp.float32)
        pieces = (
            lax.all_gather(real_low, "col", axis=1, tiled=True),
            lax.all_gather(imag_low, "col", axis=1, tiled=True),
        )
        strip = ham_columns
        right_real = jnp.dot(pieces[0], strip, preferred_element_type=jnp.float32)
        right_imag = jnp.dot(pieces[1], strip, preferred_element_type=jnp.float32)
        matrix = jnp.stack([real_part, imag_part])
        padded = extended(matrix.astype(jnp.bfloat16), (("row", 1), ("col", 2)), OMAX).astype(
            matrix.dtype
        )
        loss = dissipate(matrix, padded, amplitudes, offsets, active, row_first, col_first)
        return (left_imag - right_imag + loss[0], right_real - left_real + loss[1])

    first_real, first_imag = drift(rho_real, rho_imag)
    middle_real = rho_real + step_size * first_real
    middle_imag = rho_imag + step_size * first_imag
    rescale = levels / start_trace
    middle_real = middle_real * rescale
    middle_imag = middle_imag * rescale
    second_real, second_imag = drift(middle_real, middle_imag)
    updated_real = rho_real + 0.5 * step_size * (first_real + second_real)
    updated_imag = rho_imag + 0.5 * step_size * (first_imag + second_imag)
    rescale = levels / start_trace
    return (updated_real * rescale, updated_imag * rescale)


def solution(mesh):
    in_specs = (P("row", "col"), P("row", "col"), P("row", "col"), P(), P(), P())
    out_specs = (P("row", "col"), P("row", "col"))
    return jax.shard_map(local, mesh=mesh, in_specs=in_specs, out_specs=out_specs, check_vma=False)
```

profile of v0, /device:TPU:0, one launch (start us, length us, event | category | flops | bytes accessed | tf_op | source)
XLA Modules:
  0.0 739.2 jit_solution(2727342368948847065)
XLA Ops:
  7.2 2.7 convert_element_type.41
  15.4 4.9 collective-permute-start
  63.5 47.8 %psum.7 = f32[]{:T(128)} all-reduce(f32[]{:T(128)} %select_reduce_fusion), channel_id=1, replica_groups=mesh['row'=4,'col'=8] {'row','col'}, use_global_device_ids=true, to_apply=%region_1.2 | all-reduce | flops 1 | bytes 8 | tf_op jit(solution)/shard_map/psum | solution.py:69
  128.4 5.1 maximum_convert_fusion
  133.5 28.7 %select_add_fusion.1 = f32[2,1024,512]{2,1,0:T(8,128)} fusion(f32[2,1056,544]{2,1,0:T(8,128)} %maximum_convert_fusion, s32[]{:T(128)S(6)} %select_n.358, s32[]{:T(128)S(6)} %select_n.359, s32[]{:T(128)S(6)} %select_n.351, s32[]{:T(128)S(6)} %select_n.352, s32[]{:T(128)S(6)} %select_n.344, s32[]{:T(128)S(6)} %select_n.345, s32[]{:T(128)S(6)} %select_n.337, ...), kind=kLoop, calls=%fused_computation.3 | loop fusion | flops 41943040 | bytes 75497544 | tf_op jit(solution)/shard_map/add | solution.py:52
  162.2 10.7 %fusion.70 = f32[1024,512]{1,0:T(8,128)} fusion(bf16[1024,4096]{1,0:T(8,128)(2,1)} %all-gather.11.cloned.1.call-done, bf16[4096,512]{1,0:T(8,128)(2,1)} %all-gather.13.cloned.1.call-done), kind=kOutput, calls=%fused_computation.125 | convolution fusion | flops 4294967296 | bytes 14680064 | tf_op jit(solution)/shard_map/dot_general | solution.py:81
  172.9 61.2 %all-gather.17.cloned.1.call-done = bf16[4096,512]{1,0:T(8,128)(2,1)} async-done(((bf16[1024,512]{1,0:T(8,128)(2,1)}), bf16[4096,512]{1,0:T(8,128)(2,1)}) %all-gather.17.cloned.1.call-update) | async-done | bytes 4194320 | tf_op jit(solution)/shard_map/all_gather | solution.py:68
  234.0 56.1 %all-gather.15.cloned.1.call-done = bf16[1024,4096]{1,0:T(8,128)(2,1)} async-done(((bf16[1024,512]{1,0:T(8,128)(2,1)}), bf16[1024,4096]{1,0:T(8,128)(2,1)}) %all-gather.15.cloned.1.call-update) | async-done | bytes 8388624 | tf_op jit(solution)/shard_map/all_gather | solution.py:84
  290.2 10.5 %fusion.13 = f32[1024,512]{1,0:T(8,128)S(1)} fusion(f32[2,1024,512]{2,1,0:T(8,128)} %select_add_fusion.1, f32[1024,512]{1,0:T(8,128)} %fusion.70, bf16[1024,4096]{1,0:T(8,128)(2,1)} %all-gather.15.cloned.1.call-done, bf16[4096,512]{1,0:T(8,128)(2,1)} %all-gather.17.cloned.1.call-done), kind=kOutput, calls=%fused_computation.23 | convolution fusion | flops 4296015872 | bytes 18874368 | tf_op jit(solution)/shard_map/dot_general | solution.py:88
  305.7 53.7 %all-gather.19.cloned.1.call-done = bf16[1024,4096]{1,0:T(8,128)(2,1)} async-done(((bf16[1024,512]{1,0:T(8,128)(2,1)}), bf16[1024,4096]{1,0:T(8,128)(2,1)}) %all-gather.19.cloned.1.call-update) | async-done | bytes 8388624 | tf_op jit(solution)/shard_map/all_gather | solution.py:83
  359.4 10.5 %fusion.71 = f32[1024,512]{1,0:T(8,128)} fusion(bf16[1024,4096]{1,0:T(8,128)(2,1)} %all-gather.19.cloned.1.call-done, bf16[4096,512]{1,0:T(8,128)(2,1)} %all-gather.17.cloned.1.call-done), kind=kOutput, calls=%fused_computation.126 | convolution fusion | flops 4294967296 | bytes 14680064 | tf_op jit(solution)/shard_map/dot_general | solution.py:87
  369.8 71.7 %all-gather.21.cloned.1.call-done = bf16[4096,512]{1,0:T(8,128)(2,1)} async-done(((bf16[1024,512]{1,0:T(8,128)(2,1)}), bf16[4096,512]{1,0:T(8,128)(2,1)}) %all-gather.21.cloned.1.call-update) | async-done | bytes 4194320 | tf_op jit(solution)/shard_map/all_gather | solution.py:76
  441.6 10.3 %fusion.12 = f32[1024,512]{1,0:T(8,128)S(1)} fusion(f32[2,1024,512]{2,1,0:T(8,128)} %select_add_fusion.1, f32[1024,512]{1,0:T(8,128)} %fusion.71, bf16[1024,4096]{1,0:T(8,128)(2,1)} %all-gather.11.cloned.1.call-done, bf16[4096,512]{1,0:T(8,128)(2,1)} %all-gather.21.cloned.1.call-done), kind=kOutput, calls=%fused_computation.21 | convolution fusion | flops 4296015872 | bytes 18874368 | tf_op jit(solution)/shard_map/dot_general | solution.py:80
  461.3 4.3 collective-permute-done.5
  470.1 27.8 %all-gather.27.cloned.1.call-done = bf16[1024,4096]{1,0:T(8,128)(2,1)} async-done(((bf16[1024,512]{1,0:T(8,128)(2,1)}), bf16[1024,4096]{1,0:T(8,128)(2,1)}) %all-gather.27.cloned.1.call-update) | async-done | bytes 8388624 | tf_op jit(solution)/shard_map/all_gather | solution.py:83
  497.9 10.4 %fusion.73 = f32[1024,512]{1,0:T(8,128)} fusion(bf16[1024,4096]{1,0:T(8,128)(2,1)} %all-gather.27.cloned.1.call-done, bf16[4096,512]{1,0:T(8,128)(2,1)} %all-gather.17.cloned.1.call-done), kind=kOutput, calls=%fused_computation.128 | convolution fusion | flops 4294967296 | bytes 14680064 | tf_op jit(solution)/shard_map/dot_general | solution.py:87
  508.9 5.4 maximum_convert_fusion.1
  514.3 29.5 %select_add_fusion = f32[2,1024,512]{2,1,0:T(8,128)} fusion(f32[2,1056,544]{2,1,0:T(8,128)} %maximum_convert_fusion.1, s32[]{:T(128)S(6)} %select_n.358, s32[]{:T(128)S(6)} %select_n.359, s32[]{:T(128)S(6)} %select_n.351, s32[]{:T(128)S(6)} %select_n.352, s32[]{:T(128)S(6)} %select_n.344, s32[]{:T(128)S(6)} %select_n.345, s32[]{:T(128)S(6)} %select_n.337, ...), kind=kLoop, calls=%fused_computation.2 | loop fusion | flops 41943040 | bytes 75497544 | tf_op jit(solution)/shard_map/add | solution.py:52
  543.8 37.2 %all-gather.29.cloned.1.call-done = bf16[4096,512]{1,0:T(8,128)(2,1)} async-done(((bf16[1024,512]{1,0:T(8,128)(2,1)}), bf16[4096,512]{1,0:T(8,128)(2,1)}) %all-gather.29.cloned.1.call-update) | async-done | bytes 4194320 | tf_op jit(solution)/shard_map/all_gather | solution.py:76
  581.0 12.5 %fusion.6 = f32[1024,512]{1,0:T(8,128)} fusion(f32[1024,512]{1,0:T(8,128)S(1)} %copy-done, f32[1024,512]{1,0:T(8,128)} %copy-done.8, f32[2,1024,512]{2,1,0:T(8,128)} %select_add_fusion, f32[1024,512]{1,0:T(8,128)} %fusion.73, bf16[1024,4096]{1,0:T(8,128)(2,1)} %all-gather.11.cloned.1.call-done, bf16[4096,512]{1,0:T(8,128)(2,1)} %all-gather.29.cloned.1.call-done, ...), kind=kOutput, calls=%fused_computation.13 | convolution fusion | flops 4298113024 | bytes 23068676 | tf_op jit(solution)/shard_map/dot_general | solution.py:80
  593.4 43.8 %all-gather.25.cloned.1.call-done = bf16[1024,4096]{1,0:T(8,128)(2,1)} async-done(((bf16[1024,512]{1,0:T(8,128)(2,1)}), bf16[1024,4096]{1,0:T(8,128)(2,1)}) %all-gather.25.cloned.1.call-update) | async-done | bytes 8388624 | tf_op jit(solution)/shard_map/all_gather | solution.py:84
  637.2 10.5 %fusion.72 = f32[1024,512]{1,0:T(8,128)} fusion(bf16[1024,4096]{1,0:T(8,128)(2,1)} %all-gather.25.cloned.1.call-done, bf16[4096,512]{1,0:T(8,128)(2,1)} %all-gather.17.cloned.1.call-done), kind=kOutput, calls=%fused_computation.127 | convolution fusion | flops 4294967296 | bytes 14680064 | tf_op jit(solution)/shard_map/dot_general | solution.py:88
  647.7 71.7 %all-gather.23.cloned.1.call-done = bf16[4096,512]{1,0:T(8,128)(2,1)} async-done(((bf16[1024,512]{1,0:T(8,128)(2,1)}), bf16[4096,512]{1,0:T(8,128)(2,1)}) %all-gather.23.cloned.1.call-update) | async-done | bytes 4194320 | tf_op jit(solution)/shard_map/all_gather | solution.py:77
  719.4 12.5 %fusion.11 = f32[1024,512]{1,0:T(8,128)} fusion(f32[1024,512]{1,0:T(8,128)S(1)} %copy-done.3, f32[1024,512]{1,0:T(8,128)} %copy-done.7, f32[2,1024,512]{2,1,0:T(8,128)} %select_add_fusion, f32[1024,512]{1,0:T(8,128)} %fusion.72, bf16[1024,4096]{1,0:T(8,128)(2,1)} %all-gather.11.cloned.1.call-done, bf16[4096,512]{1,0:T(8,128)(2,1)} %all-gather.23.cloned.1.call-done, ...), kind=kOutput, calls=%fused_computation.19 | convolution fusion | flops 4298113024 | bytes 23068676 | tf_op jit(solution)/shard_map/dot_general | solution.py:81
  (127 shorter events, 58.2 us)
Async XLA Ops:
  7.2 155.0 %all-gather.13.cloned.1.call-start = ((), (), s32[]{:S(2)}) async-start(), calls=%async_computation.1 | async-start | bytes 5242880 | tf_op jit(solution)/shard_map/all_gather | solution.py:77
  10.0 152.2 %all-gather.11.cloned.1.call-start = ((), (), s32[]{:S(2)}) async-start(), calls=%async_computation | async-start | bytes 9437184 | tf_op jit(solution)/shard_map/all_gather | solution.py:74
  10.7 223.3 %all-gather.17.cloned.1.call-start = ((), (), s32[]{:S(2)}) async-start(), calls=%async_computation.3 | async-start | bytes 5242880 | tf_op jit(solution)/shard_map/all_gather | solution.py:68
  11.4 278.7 %all-gather.15.cloned.1.call-start = ((), (), s32[]{:S(2)}) async-start(), calls=%async_computation.2 | async-start | bytes 9437184 | tf_op jit(solution)/shard_map/all_gather | solution.py:84
  12.0 347.4 %all-gather.19.cloned.1.call-start = ((), (), s32[]{:S(2)}) async-start(), calls=%async_computation.4 | async-start | bytes 9437184 | tf_op jit(solution)/shard_map/all_gather | solution.py:83
  12.1 9.6 %copy-start.10 = (s32[8]{0:T(128)S(1)}, s32[8]{0:T(128)}, u32[]{:S(2)}) copy-start(s32[8]{0:T(128)} %param.10) | copy-start | bytes 100
  12.1 20.4 %copy-start.9 = (f32[8,4096]{1,0:T(8,128)S(1)}, f32[8,4096]{1,0:T(8,128)}, u32[]{:S(2)}) copy-start(f32[8,4096]{1,0:T(8,128)} %param.9) | copy-start | bytes 393220
  15.4 42.2 %collective-permute-start = (bf16[2,16,512]{2,1,0:T(8,128)(2,1)S(1)}, bf16[2,16,512]{2,1,0:T(8,128)(2,1)S(1)}, u32[]{:S(2)}, u32[]{:S(2)}) collective-permute-start(bf16[2,16,512]{2,1,0:T(8,128)(2,1)S(1)} %get-tuple-element.29), channel_id=1, source_target_pairs={{0,8},{8,16},{16,24},{1,9},{9,17},{17,25},{2,10},{10,18},{18,26},{... | collective-permute-start | bytes 98312 | tf_op jit(solution)/shard_map/ppermute | solution.py:20
  20.4 37.3 %collective-permute-start.1 = (bf16[2,16,512]{2,1,0:T(8,128)(2,1)S(1)}, bf16[2,16,512]{2,1,0:T(8,128)(2,1)S(1)}, u32[]{:S(2)}, u32[]{:S(2)}) collective-permute-start(bf16[2,16,512]{2,1,0:T(8,128)(2,1)S(1)} %get-tuple-element.30), channel_id=1, source_target_pairs={{8,0},{16,8},{24,16},{9,1},{17,9},{25,17},{10,2},{18,10},{26,18},{... | collective-permute-start | bytes 98312 | tf_op jit(solution)/shard_map/ppermute | solution.py:22
  53.7 3.9 copy-start.5
  58.1 69.7 %collective-permute-start.2 = (bf16[2,1056,16]{1,2,0:T(8,128)(2,1)S(1)}, bf16[2,1056,16]{1,2,0:T(8,128)(2,1)S(1)}, u32[]{:S(2)}, u32[]{:S(2)}) collective-permute-start(bf16[2,1056,16]{1,2,0:T(8,128)(2,1)S(1)} %copy.10), channel_id=1, source_target_pairs={{0,1},{1,2},{2,3},{3,4},{4,5},{5,6},{6,7},{8,9},{9,10},{10,11},{11... | collective-permute-start | bytes 202760 | tf_op jit(solution)/shard_map/ppermute | solution.py:20
  59.8 68.3 %collective-permute-start.3 = (bf16[2,1056,16]{1,2,0:T(8,128)(2,1)S(1)}, bf16[2,1056,16]{1,2,0:T(8,128)(2,1)S(1)}, u32[]{:S(2)}, u32[]{:S(2)}) collective-permute-start(bf16[2,1056,16]{1,2,0:T(8,128)(2,1)S(1)} %copy.11), channel_id=1, source_target_pairs={{1,0},{2,1},{3,2},{4,3},{5,4},{6,5},{7,6},{9,8},{10,9},{11,10},{12... | collective-permute-start | bytes 202760 | tf_op jit(solution)/shard_map/ppermute | solution.py:22
  290.2 10.5 %copy-start.2 = (f32[1024,512]{1,0:T(8,128)S(1)}, f32[1024,512]{1,0:T(8,128)}, u32[]{:S(2)}) copy-start(f32[1024,512]{1,0:T(8,128)} %param.6) | copy-start | bytes 6291460
  300.6 2.7 copy-start.7
  303.4 138.2 %all-gather.21.cloned.1.call-start = ((), (), s32[]{:S(2)}) async-start(), calls=%async_computation.5 | async-start | bytes 5242880 | tf_op jit(solution)/shard_map/all_gather | solution.py:76
  303.9 194.0 %all-gather.27.cloned.1.call-start = ((), (), s32[]{:S(2)}) async-start(), calls=%async_computation.8 | async-start | bytes 9437184 | tf_op jit(solution)/shard_map/all_gather | solution.py:83
  304.7 276.3 %all-gather.29.cloned.1.call-start = ((), (), s32[]{:S(2)}) async-start(), calls=%async_computation.9 | async-start | bytes 5242880 | tf_op jit(solution)/shard_map/all_gather | solution.py:76
  305.4 331.8 %all-gather.25.cloned.1.call-start = ((), (), s32[]{:S(2)}) async-start(), calls=%async_computation.7 | async-start | bytes 9437184 | tf_op jit(solution)/shard_map/all_gather | solution.py:84
  454.4 265.0 %all-gather.23.cloned.1.call-start = ((), (), s32[]{:S(2)}) async-start(), calls=%async_computation.6 | async-start | bytes 5242880 | tf_op jit(solution)/shard_map/all_gather | solution.py:77
  458.4 2.9 collective-permute-start.4
  459.7 5.9 collective-permute-start.5
  467.3 41.0 %collective-permute-start.6 = (bf16[2,1056,16]{1,2,0:T(8,128)(2,1)S(1)}, bf16[2,1056,16]{1,2,0:T(8,128)(2,1)S(1)}, u32[]{:S(2)}, u32[]{:S(2)}) collective-permute-start(bf16[2,1056,16]{1,2,0:T(8,128)(2,1)S(1)} %copy.15), channel_id=1, source_target_pairs={{0,1},{1,2},{2,3},{3,4},{4,5},{5,6},{6,7},{8,9},{9,10},{10,11},{11... | collective-permute-start | bytes 202760 | tf_op jit(solution)/shard_map/ppermute | solution.py:20
  468.8 39.8 %collective-permute-start.7 = (bf16[2,1056,16]{1,2,0:T(8,128)(2,1)S(1)}, bf16[2,1056,16]{1,2,0:T(8,128)(2,1)S(1)}, u32[]{:S(2)}, u32[]{:S(2)}) collective-permute-start(bf16[2,1056,16]{1,2,0:T(8,128)(2,1)S(1)} %copy.16), channel_id=1, source_target_pairs={{1,0},{2,1},{3,2},{4,3},{5,4},{6,5},{7,6},{9,8},{10,9},{11,10},{12... | collective-permute-start | bytes 202760 | tf_op jit(solution)/shard_map/ppermute | solution.py:22
  593.4 126.0 %copy-start.3 = (f32[1024,512]{1,0:T(8,128)S(1)}, f32[1024,512]{1,0:T(8,128)}, u32[]{:S(2)}) copy-start(f32[1024,512]{1,0:T(8,128)} %param.6) | copy-start | bytes 6291460
  (5 other events, 9.8 us)
Sparse Core Ops, SparseCore 0:
  10.1 84.7 all-gather.12
  96.8 54.8 all-gather.10
  153.3 80.7 all-gather.16
  235.8 54.3 all-gather.14
  303.5 55.8 all-gather.18
  360.8 80.7 all-gather.20
  443.4 54.4 all-gather.26
  499.5 81.4 all-gather.28
  582.8 54.3 all-gather.24
  638.6 80.7 all-gather.22
where the time goes:
time: 745 us; the launch traced here: 739 us
  waiting for transfers between devices  432 us (58%)
  other arithmetic  108 us (14%)
  matrix products  87.7 us (12%)
  blocking collectives  47.8 us (6%)
  between operations  41.6 us (6%)
  starting transfers between devices  14.8 us (2%)
    all_gather x2, waiting for transfers between devices, drift(): lax.all_gather(real_low, 'row', axis=0, tiled=True)  109 us
    all_gather x2, waiting for transfers between devices, drift(): lax.all_gather(imag_low, 'col', axis=1, tiled=True)  99.9 us
    all_gather x2, waiting for transfers between devices, drift(): lax.all_gather(real_low, 'col', axis=1, tiled=True)  81.5 us
    all_gather x2, waiting for transfers between devices, drift(): lax.all_gather(imag_low, 'row', axis=0, tiled=True)  71.7 us
    all_gather x1, waiting for transfers between devices, local(): ham_columns = lax.all_gather(hamiltonian, 'row', axis=0, tiled=True)  61.2 us
    add x2, other arithmetic, dissipate(): summed = summed + jnp.where(jump_slot < active, contribution, 0.0)  58.1 us
    psum x1, blocking collectives, local(): lax.psum(diagonal_sum(rho_real, row_first, col_first), ('row', 'col'))  47.8 us
    dot_general x2, matrix products, drift(): left_imag = jnp.dot(strip, pieces[1], preferred_element_type=jnp.float32)  23.1 us
  transfers between devices with their start and end apart: 18, of which 10 were waited for; matrix products, arithmetic and copies ran while one was open for 23% of the time, Pallas kernels for 0%

commit v1 on v0

--- a/solution.py
+++ b/solution.py
@@ -1,12 +1,300 @@
+import functools
+
 import jax
 import jax.numpy as jnp
 from jax import lax
+from jax.experimental import pallas as pl
+from jax.experimental.pallas import tpu as pltpu
 from jax.sharding import PartitionSpec as P
 
 OMAX = 16
 
 
 step_size = 0.25
+
+VMEM_LIMIT = 62 * 1024 * 1024
+
+
+def ring_plan(count, favour_up):
+    far = count // 2
+    near = count - 1 - far
+    return (far, near) if favour_up else (near, far)
+
+
+def top(mask):
+    return mask.bit_length() - 1
+
+
+def commutator_kernel(first, nz, nc, *refs):
+    if first:
+        (real, imag, ham, out_real, out_imag, ham_rows_out, ham_cols_out,
+         ham_rows, ham_cols, real_rows, imag_rows, real_cols, imag_cols,
+         xy_send, xy_recv, z_send, z_recv, local_sem) = refs
+    else:
+        (real, imag, ham_rows_in, ham_cols_in, out_real, out_imag,
+         ham_rows, ham_cols, real_rows, imag_rows, real_cols, imag_cols,
+         xy_send, xy_recv, z_send, z_recv, local_sem) = refs
+        ham = None
+    height, breadth = real.shape
+    z = lax.axis_index("row")
+    c = lax.axis_index("col")
+    bits = nc.bit_length() - 1
+    half = height // 2
+    physical = list(range(1, bits))
+    order_a = physical + [0]
+    order_b = physical[::-1] + [0]
+
+    pieces = []
+    if first:
+        pieces.append((ham, ham_rows, (0, half), order_a))
+        pieces.append((ham, ham_rows, (half, half), order_b))
+    pieces.append((real, real_rows, (0, height), order_a))
+    pieces.append((imag, imag_rows, (0, height), order_b))
+    rings = []
+    if first:
+        rings.append((ham, ham_cols, (0, half), True))
+        rings.append((ham, ham_cols, (half, half), False))
+    rings.append((real, real_cols, (0, height), True))
+    rings.append((imag, imag_cols, (0, height), False))
+
+    barrier = pltpu.get_barrier_semaphore()
+    up = lax.rem(z + 1, nz)
+    down = lax.rem(z + nz - 1, nz)
+
+    def flip(index, b):
+        weight = 1 << b
+        bit = lax.rem(index // weight, 2)
+        return index + weight * (1 - 2 * bit)
+
+    def masked(mask, order):
+        index = c
+        for t in range(bits):
+            if mask >> t & 1:
+                index = flip(index, order[t])
+        return index
+
+    for neighbour in (up, down):
+        pl.semaphore_signal(barrier, inc=1, device_id=(neighbour, c), device_id_type=pl.DeviceIdType.MESH)
+    for b in range(bits):
+        pl.semaphore_signal(barrier, inc=1, device_id=(z, flip(c, b)), device_id_type=pl.DeviceIdType.MESH)
+    pl.semaphore_wait(barrier, 2 + bits)
+
+    def xy_copy(p, mask, t):
+        own, panel, (start, size), order = pieces[p]
+        index = masked(mask, order)
+        rows = pl.ds(start, size)
+        source = own.at[rows, :] if mask == 0 else panel.at[index, rows, :]
+        arrival = mask | 1 << t
+        return pltpu.make_async_remote_copy(
+            src_ref=source,
+            dst_ref=panel.at[index, rows, :],
+            send_sem=xy_send.at[p, arrival],
+            recv_sem=xy_recv.at[p, arrival],
+            device_id=(z, flip(c, order[t])),
+            device_id_type=pl.DeviceIdType.MESH,
+        )
+
+    def z_copy(p, direction, step):
+        own, panel, (start, size), _ = rings[p]
+        rows = pl.ds(start, size)
+        shift = nz - (step - 1) if direction == 0 else step - 1
+        index = lax.rem(z + shift, nz)
+        source = own.at[rows, :] if step == 1 else panel.at[index, rows, :]
+        return pltpu.make_async_remote_copy(
+            src_ref=source,
+            dst_ref=panel.at[index, rows, :],
+            send_sem=z_send.at[p, direction, step],
+            recv_sem=z_recv.at[p, direction, step],
+            device_id=(up if direction == 0 else down, c),
+            device_id_type=pl.DeviceIdType.MESH,
+        )
+
+    started = []
+
+    def begin(copy):
+        copy.start()
+        started.append(copy)
+
+    for p in range(len(pieces)):
+        for t in range(bits):
+            begin(xy_copy(p, 0, t))
+    for p in range(len(rings)):
+        plan = ring_plan(nz, rings[p][3])
+        for direction in (0, 1):
+            if plan[direction] >= 1:
+                begin(z_copy(p, direction, 1))
+
+    if first:
+        locals_in = [
+            pltpu.make_async_copy(ham, ham_rows.at[c], local_sem.at[0]),
+            pltpu.make_async_copy(ham, ham_cols.at[z], local_sem.at[1]),
+        ]
+    else:
+        locals_in = [
+            pltpu.make_async_copy(ham_rows_in, ham_rows, local_sem.at[0]),
+            pltpu.make_async_copy(ham_cols_in, ham_cols, local_sem.at[1]),
+        ]
+    for copy in locals_in:
+        copy.start()
+
+    def advance_xy(p, mask):
+        order_t = top(mask)
+        xy_copy(p, mask & ~(1 << order_t), order_t).wait_recv()
+        for t in range(order_t + 1, bits):
+            begin(xy_copy(p, mask, t))
+
+    def advance_z(p, direction, step):
+        plan = ring_plan(nz, rings[p][3])
+        z_copy(p, direction, step).wait_recv()
+        if step < plan[direction]:
+            begin(z_copy(p, direction, step + 1))
+
+    ring_steps = max(ring_plan(nz, True))
+
+    def ring_events(p, step):
+        plan = ring_plan(nz, rings[p][3])
+        return [(p, d, step) for d in (0, 1) if step <= plan[d]]
+
+    base = 0
+    if first:
+        base = 2
+        for mask in range(1, nc):
+            for p in (0, 1):
+                advance_xy(p, mask)
+            if mask <= ring_steps:
+                for p in (0, 1):
+                    for event in ring_events(p, mask):
+                        advance_z(*event)
+        for step in range(nc, ring_steps + 1):
+            for p in (0, 1):
+                for event in ring_events(p, step):
+                    advance_z(*event)
+    for copy in locals_in:
+        copy.wait()
+    outs = []
+    if first:
+        outs = [
+            pltpu.make_async_copy(ham_rows, ham_rows_out, local_sem.at[0]),
+            pltpu.make_async_copy(ham_cols, ham_cols_out, local_sem.at[1]),
+        ]
+        for copy in outs:
+            copy.start()
+
+    per = height // breadth
+    tile = min(256, height)
+
+    def rows_product(out, block, index, sign, fresh):
+        k = index // per
+        offset = pl.multiple_of(lax.rem(index, per) * breadth, breadth)
+
+        @pl.loop(0, height // tile)
+        def _(i):
+            here = pl.ds(pl.multiple_of(i * tile, tile), tile)
+            product = jnp.dot(
+                block[here, :], ham_cols[k, pl.ds(offset, breadth), :], preferred_element_type=jnp.float32
+            )
+            if fresh:
+                out[here, :] = product if sign > 0 else -product
+            elif sign > 0:
+                out[here, :] += product
+            else:
+                out[here, :] -= product
+
+    def cols_product(out, block, k, sign):
+        @pl.loop(0, height // tile)
+        def _(i):
+            here = pl.ds(pl.multiple_of(i * tile, tile), tile)
+            product = jnp.dot(
+                ham_rows[k * per, here, :], block[pl.ds(0, breadth), :], preferred_element_type=jnp.float32
+            )
+            for part in range(1, per):
+                product += jnp.dot(
+                    ham_rows[k * per + part, here, :],
+                    block[pl.ds(part * breadth, breadth), :],
+                    preferred_element_type=jnp.float32,
+                )
+            if sign > 0:
+                out[here, :] += product
+            else:
+                out[here, :] -= product
+
+    rows_product(out_imag, real, c, 1, True)
+    rows_product(out_real, imag, c, -1, True)
+    cols_product(out_imag, real, z, -1)
+    cols_product(out_real, imag, z, 1)
+    sides = ((real_rows, real_cols, out_imag, 1), (imag_rows, imag_cols, out_real, -1))
+
+    def consume_ring(step):
+        for side, (_, cols, out, sign) in enumerate(sides):
+            for p, direction, s in ring_events(base + side, step):
+                advance_z(p, direction, s)
+                shift = nz - s if direction == 0 else s
+                k = lax.rem(z + shift, nz)
+                cols_product(out, cols.at[k], k, -sign)
+
+    done_steps = 0
+    for mask in range(1, nc):
+        for side, (rows, _, out, sign) in enumerate(sides):
+            p = base + side
+            advance_xy(p, mask)
+        for side, (rows, _, out, sign) in enumerate(sides):
+            index = masked(mask, pieces[base + side][3])
+            rows_product(out, rows.at[index], index, sign, False)
+        want = mask * ring_steps // (nc - 1) if nc > 1 else ring_steps
+        while done_steps < want:
+            done_steps += 1
+            consume_ring(done_steps)
+    for copy in started:
+        copy.wait_send()
+    for copy in outs:
+        copy.wait()
+
+
+def commutator(real_low, imag_low, ham, panels, nz, nc):
+    height, breadth = real_low.shape
+    first = panels is None
+    vmem = pl.BlockSpec(memory_space=pltpu.VMEM)
+    anywhere = pl.BlockSpec(memory_space=pl.ANY)
+    drift_shape = jax.ShapeDtypeStruct((height, breadth), jnp.float32)
+    low = jnp.bfloat16
+    rows_shape = (nc, height, breadth)
+    cols_shape = (nz, height, breadth)
+    out_shape = [drift_shape, drift_shape]
+    out_specs = [vmem, vmem]
+    if first:
+        out_shape += [jax.ShapeDtypeStruct(rows_shape, low), jax.ShapeDtypeStruct(cols_shape, low)]
+        out_specs += [anywhere, anywhere]
+        in_specs = [vmem] * 3
+        operands = (real_low, imag_low, ham)
+    else:
+        in_specs = [vmem, vmem, anywhere, anywhere]
+        operands = (real_low, imag_low) + tuple(panels)
+    count = 4 if first else 2
+    flops = 8 * height * breadth * nz * height
+    return pl.pallas_call(
+        functools.partial(commutator_kernel, first, nz, nc),
+        out_shape=out_shape,
+        in_specs=in_specs,
+        out_specs=out_specs,
+        scratch_shapes=[
+            pltpu.VMEM(rows_shape, low),
+            pltpu.VMEM(cols_shape, low),
+            pltpu.VMEM(rows_shape, low),
+            pltpu.VMEM(rows_shape, low),
+            pltpu.VMEM(cols_shape, low),
+            pltpu.VMEM(cols_shape, low),
+            pltpu.SemaphoreType.DMA((count, nc)),
+            pltpu.SemaphoreType.DMA((count, nc)),
+            pltpu.SemaphoreType.DMA((count, 2, nz)),
+            pltpu.SemaphoreType.DMA((count, 2, nz)),
+            pltpu.SemaphoreType.DMA((2,)),
+        ],
+        compiler_params=pltpu.CompilerParams(
+            collective_id=0 if first else 1, has_side_effects=True, vmem_limit_bytes=VMEM_LIMIT
+        ),
+        cost_estimate=pl.CostEstimate(flops=flops, bytes_accessed=16 * height * breadth, transcendentals=0),
+        name="first_commutator" if first else "second_commutator",
+    )(*operands)
 
 
 def extended(cells, sides, width):
@@ -59,54 +347,37 @@
     return jnp.sum(jnp.where(row_index == col_index, matrix, 0.0))
 
 
-def local(rho_real, rho_imag, hamiltonian, amplitudes, offsets, active_jumps):
+def local(nz, nc, rho_real, rho_imag, hamiltonian, amplitudes, offsets, active_jumps):
     height, breadth = rho_real.shape
     levels = amplitudes.shape[1]
     row_first = lax.axis_index("row") * height
     col_first = lax.axis_index("col") * breadth
     active = active_jumps[0]
-    ham_columns = lax.all_gather(hamiltonian, "row", axis=0, tiled=True)
     start_trace = lax.psum(diagonal_sum(rho_real, row_first, col_first), ("row", "col"))
 
-    def drift(real_part, imag_part):
+    def drift(real_part, imag_part, panels):
         real_low = real_part.astype(jnp.bfloat16)
         imag_low = imag_part.astype(jnp.bfloat16)
-        row_panel = lax.all_gather(hamiltonian, "col", axis=1, tiled=True)
-        pieces = (
-            lax.all_gather(real_low, "row", axis=0, tiled=True),
-            lax.all_gather(imag_low, "row", axis=0, tiled=True),
-        )
-        strip = row_panel
-        left_real = jnp.dot(strip, pieces[0], preferred_element_type=jnp.float32)
-        left_imag = jnp.dot(strip, pieces[1], preferred_element_type=jnp.float32)
-        pieces = (
-            lax.all_gather(real_low, "col", axis=1, tiled=True),
-            lax.all_gather(imag_low, "col", axis=1, tiled=True),
-        )
-        strip = ham_columns
-        right_real = jnp.dot(pieces[0], strip, preferred_element_type=jnp.float32)
-        right_imag = jnp.dot(pieces[1], strip, preferred_element_type=jnp.float32)
+        real_turn, imag_turn, *made = commutator(real_low, imag_low, hamiltonian, panels, nz, nc)
         matrix = jnp.stack([real_part, imag_part])
         padded = extended(matrix.astype(jnp.bfloat16), (("row", 1), ("col", 2)), OMAX).astype(
             matrix.dtype
         )
         loss = dissipate(matrix, padded, amplitudes, offsets, active, row_first, col_first)
-        return (left_imag - right_imag + loss[0], right_real - left_real + loss[1])
-
-    first_real, first_imag = drift(rho_real, rho_imag)
-    middle_real = rho_real + step_size * first_real
-    middle_imag = rho_imag + step_size * first_imag
+        return real_turn + loss[0], imag_turn + loss[1], made
+
+    first_real, first_imag, panels = drift(rho_real, rho_imag, None)
     rescale = levels / start_trace
-    middle_real = middle_real * rescale
-    middle_imag = middle_imag * rescale
-    second_real, second_imag = drift(middle_real, middle_imag)
+    middle_real = (rho_real + step_size * first_real) * rescale
+    middle_imag = (rho_imag + step_size * first_imag) * rescale
+    second_real, second_imag, _ = drift(middle_real, middle_imag, panels)
     updated_real = rho_real + 0.5 * step_size * (first_real + second_real)
     updated_imag = rho_imag + 0.5 * step_size * (first_imag + second_imag)
-    rescale = levels / start_trace
     return (updated_real * rescale, updated_imag * rescale)
 
 
 def solution(mesh):
     in_specs = (P("row", "col"), P("row", "col"), P("row", "col"), P(), P(), P())
     out_specs = (P("row", "col"), P("row", "col"))
-    return jax.shard_map(local, mesh=mesh, in_specs=in_specs, out_specs=out_specs, check_vma=False)
+    body = functools.partial(local, mesh.shape["row"], mesh.shape["col"])
+    return jax.shard_map(body, mesh=mesh, in_specs=in_specs, out_specs=out_specs, check_vma=False)

time: 745 us -> 619 us (0.83)
  waiting for transfers between devices: 432 us -> 4.52 us
  Pallas kernels: 0 us -> 401 us
  matrix products: 87.7 us -> 0 us
  between operations: 41.6 us -> 27.4 us
  other arithmetic: 108 us -> 117 us
  blocking collectives: 47.8 us -> 40.3 us
    all_gather x10 -> x0, waiting for transfers between devices: 423 us -> none  [the longest x2 109 us: drift(): lax.all_gather(real_low, 'row', axis=0, tiled=True)]
    pallas_call x0 -> x2, Pallas kernels: none -> 401 us  [commutator(): pl.pallas_call(functools.partial(commutator_kernel, first, nz, nc), out_s...]
    dot_general x8 -> x0, matrix products: 87.7 us -> none  [the longest x2 23.1 us: drift(): left_imag = jnp.dot(strip, pieces[1], preferred_element_type=jnp.float32)]
    mul x0 -> x1, other arithmetic: none -> 11.1 us  [local(): return (updated_real * rescale, updated_imag * rescale)]
    psum x1, blocking collectives: 47.8 us -> 40.3 us  [local(): lax.psum(diagonal_sum(rho_real, row_first, col_first), ('row', 'col'))]
  transfers between devices with their start and end apart: 18 -> 8, of which waited for: 10 -> 2; matrix products, arithmetic and copies ran while one was open for 23% -> 5% of each run, Pallas kernels for 0% -> 65%
where the time goes in v1:
time: 619 us; the launch traced here: 618 us
  Pallas kernels  401 us (65%)
  other arithmetic  117 us (19%)
  blocking collectives  40.3 us (7%)
  between operations  27.4 us (4%)
  starting transfers between devices  20.1 us (3%)
  local copies, waits for them, and re-layouts  7.63 us (1%)
    pallas_call x2, Pallas kernels, commutator(): pl.pallas_call(functools.partial(commutator_kernel, first, nz, nc), out_s...  401 us
    add x2, other arithmetic, dissipate(): summed = summed + jnp.where(jump_slot < active, contribution, 0.0)  57.7 us
    psum x1, blocking collectives, local(): lax.psum(diagonal_sum(rho_real, row_first, col_first), ('row', 'col'))  40.3 us
    ppermute x4, starting transfers between devices, extended(): lax.ppermute(tail, axis, [(i, (i + 1) % count) for i in range(ends)])  14.9 us
  transfers between devices with their start and end apart: 8, of which 2 were waited for; matrix products, arithmetic and copies ran while one was open for 5% of the time, Pallas kernels for 65%

profile of v1, /device:TPU:0, one launch (start us, length us, event | category | flops | bytes accessed | tf_op | source)
XLA Modules:
  0.0 618.0 jit_solution(203750400356876606)
XLA Ops:
  0.7 2.7 fusion.1
  4.7 4.9 collective-permute-start
  30.0 2.3 fusion.66
  32.3 254.5 %first_commutator.1 = (f32[1024,512]{1,0:T(8,128)}, f32[1024,512]{1,0:T(8,128)}, bf16[8,1024,512]{2,1,0:T(8,128)(2,1)}, bf16[4,1024,512]{2,1,0:T(8,128)(2,1)}) custom-call(bf16[1024,512]{1,0:T(8,128)(2,1)} %get-tuple-element.46.refs_0_, bf16[1024,512]{1,0:T(8,128)(2,1)} %convert_element_type.42.refs_1_, bf16[1024,512]{1,0:T(8,128)(2,1)} %refs_2_.1), custom_call_target="tpu_custom_call" | custom-call | flops 17179869184 | bytes 8388608 | tf_op jit(solution)/shard_map/first_commutator/pallas_call | solution.py:274
  286.9 2.4 broadcast_multiply_fusion
  289.3 2.4 add_multiply_fusion.2
  291.6 2.3 broadcast_multiply_fusion.6
  294.0 2.4 add_multiply_fusion.8
  296.4 2.4 broadcast_multiply_fusion.4
  298.7 2.3 add_multiply_fusion.6
  301.1 2.3 broadcast_multiply_fusion.2
  305.5 3.0 collective-permute-start.2
  308.5 2.4 add_multiply_fusion.4
  310.9 40.3 %psum.7 = f32[]{:T(128)} all-reduce(f32[]{:T(128)} %get-tuple-element.47), channel_id=1, replica_groups=mesh['row'=4,'col'=8] {'row','col'}, use_global_device_ids=true, to_apply=%region_1.2 | all-reduce | flops 1 | bytes 8 | tf_op jit(solution)/shard_map/psum | solution.py:356
  368.2 5.2 maximum_convert_fusion
  373.4 28.3 %select_add_fusion.1 = f32[2,1024,512]{2,1,0:T(8,128)} fusion(f32[2,1056,544]{2,1,0:T(8,128)} %maximum_convert_fusion, s32[]{:T(128)S(6)} %select_n.358, s32[]{:T(128)S(6)} %select_n.359, s32[]{:T(128)S(6)} %select_n.351, s32[]{:T(128)S(6)} %select_n.352, s32[]{:T(128)S(6)} %select_n.344, s32[]{:T(128)S(6)} %select_n.345, s32[]{:T(128)S(6)} %select_n.337, ...), kind=kLoop, calls=%fused_computation.3 | loop fusion | flops 41943040 | bytes 75497544 | tf_op jit(solution)/shard_map/add | solution.py:340
  401.7 7.0 %fusion.46 = (bf16[1024,512]{1,0:T(8,128)(2,1)}, f32[1024,512]{1,0:T(8,128)S(1)}, bf16[1024,512]{1,0:T(8,128)(2,1)}, f32[1024,512]{1,0:T(8,128)S(1)}) fusion(f32[]{:T(128)S(6)} %div.3, f32[1024,512]{1,0:T(8,128)S(1)} %copy-done.1, f32[1024,512]{1,0:T(8,128)} %get-tuple-element.9, f32[2,1024,512]{2,1,0:T(8,128)} %select_add_fusion.1, f32[1024,512]{1,0:T(8,128)} %param.6, ...), kind=kLoop, calls=%fused_computation.107 | loop fusion | flops 5242880 | bytes 18874372 | tf_op jit(solution)/shard_map/convert_element_type | solution.py:360
  410.7 3.6 collective-permute-start.4
  416.0 4.2 collective-permute-done.5
  422.2 3.3 collective-permute-start.6
  425.5 146.3 %second_commutator.1 = (f32[1024,512]{1,0:T(8,128)}, f32[1024,512]{1,0:T(8,128)}) custom-call(bf16[1024,512]{1,0:T(8,128)(2,1)} %get-tuple-element.36.refs_0_, bf16[1024,512]{1,0:T(8,128)(2,1)} %get-tuple-element.14.refs_1_, bf16[8,1024,512]{2,1,0:T(8,128)(2,1)} %get-tuple-element.10.refs_2_, bf16[4,1024,512]{2,1,0:T(8,128)(2,1)} %get-tuple-element.11.refs_3_), custom_call_target="tpu_custom_call" | custom-call | flops 17179869184 | bytes 8388608 | tf_op jit(solution)/shard_map/second_commutator/pallas_call | solution.py:274
  572.3 5.0 maximum_convert_fusion.1
  577.4 29.4 %select_add_fusion = f32[2,1024,512]{2,1,0:T(8,128)} fusion(f32[2,1056,544]{2,1,0:T(8,128)} %maximum_convert_fusion.1, s32[]{:T(128)S(6)} %select_n.358, s32[]{:T(128)S(6)} %select_n.359, s32[]{:T(128)S(6)} %select_n.351, s32[]{:T(128)S(6)} %select_n.352, s32[]{:T(128)S(6)} %select_n.344, s32[]{:T(128)S(6)} %select_n.345, s32[]{:T(128)S(6)} %select_n.337, ...), kind=kLoop, calls=%fused_computation.2 | loop fusion | flops 41943040 | bytes 75497544 | tf_op jit(solution)/shard_map/add | solution.py:340
  606.8 11.1 %fusion.6 = (f32[1024,512]{1,0:T(8,128)}, f32[1024,512]{1,0:T(8,128)}) fusion(f32[1024,512]{1,0:T(8,128)S(1)} %copy-done.2, f32[1024,512]{1,0:T(8,128)} %get-tuple-element.13, f32[2,1024,512]{2,1,0:T(8,128)} %select_add_fusion, f32[]{:T(128)S(6)} %div.3, f32[1024,512]{1,0:T(8,128)} %get-tuple-element.9, f32[2,1024,512]{2,1,0:T(8,128)} %select_add_fusion.1, ...), kind=kLoop, calls=%fused_computation.13 | loop fusion | flops 6291456 | bytes 25165828 | tf_op jit(solution)/shard_map/mul | solution.py:376
  (91 shorter events, 20.3 us)
Async XLA Ops:
  0.6 10.4 %copy-start.10 = (s32[8]{0:T(128)S(1)}, s32[8]{0:T(128)}, u32[]{:S(2)}) copy-start(s32[8]{0:T(128)} %param.10) | copy-start | bytes 100
  0.6 21.1 %copy-start.9 = (f32[8,4096]{1,0:T(8,128)S(1)}, f32[8,4096]{1,0:T(8,128)}, u32[]{:S(2)}) copy-start(f32[8,4096]{1,0:T(8,128)} %param.9) | copy-start | bytes 393220
  0.6 27.1 %copy-start = (f32[1024,512]{1,0:T(8,128)S(1)}, f32[1024,512]{1,0:T(8,128)}, u32[]{:S(2)}) copy-start(f32[1024,512]{1,0:T(8,128)} %param.7) | copy-start | bytes 6291460
  3.4 1.3 copy-start.4
  4.7 298.7 %collective-permute-start = (bf16[2,16,512]{2,1,0:T(8,128)(2,1)S(1)}, bf16[2,16,512]{2,1,0:T(8,128)(2,1)S(1)}, u32[]{:S(2)}, u32[]{:S(2)}) collective-permute-start(bf16[2,16,512]{2,1,0:T(8,128)(2,1)S(1)} %get-tuple-element.44), channel_id=1, source_target_pairs={{0,8},{8,16},{16,24},{1,9},{9,17},{17,25},{2,10},{10,18},{18,26},{... | collective-permute-start | bytes 98312 | tf_op jit(solution)/shard_map/ppermute | solution.py:308
  9.7 293.8 %collective-permute-start.1 = (bf16[2,16,512]{2,1,0:T(8,128)(2,1)S(1)}, bf16[2,16,512]{2,1,0:T(8,128)(2,1)S(1)}, u32[]{:S(2)}, u32[]{:S(2)}) collective-permute-start(bf16[2,16,512]{2,1,0:T(8,128)(2,1)S(1)} %get-tuple-element.45), channel_id=1, source_target_pairs={{8,0},{16,8},{24,16},{9,1},{17,9},{25,17},{10,2},{18,10},{26,18},{... | collective-permute-start | bytes 98312 | tf_op jit(solution)/shard_map/ppermute | solution.py:310
  21.7 8.3 %copy-start.3 = (f32[1024,512]{1,0:T(8,128)S(1)}, f32[1024,512]{1,0:T(8,128)}, u32[]{:S(2)}) copy-start(f32[1024,512]{1,0:T(8,128)} %param.6) | copy-start | bytes 6291460
  301.1 2.4 copy-start.5
  304.2 63.7 %collective-permute-start.3 = (bf16[2,1056,16]{1,2,0:T(8,128)(2,1)S(1)}, bf16[2,1056,16]{1,2,0:T(8,128)(2,1)S(1)}, u32[]{:S(2)}, u32[]{:S(2)}) collective-permute-start(bf16[2,1056,16]{1,2,0:T(8,128)(2,1)S(1)} %copy.9), channel_id=1, source_target_pairs={{1,0},{2,1},{3,2},{4,3},{5,4},{6,5},{7,6},{9,8},{10,9},{11,10},{12... | collective-permute-start | bytes 202760 | tf_op jit(solution)/shard_map/ppermute | solution.py:310
  305.5 62.1 %collective-permute-start.2 = (bf16[2,1056,16]{1,2,0:T(8,128)(2,1)S(1)}, bf16[2,1056,16]{1,2,0:T(8,128)(2,1)S(1)}, u32[]{:S(2)}, u32[]{:S(2)}) collective-permute-start(bf16[2,1056,16]{1,2,0:T(8,128)(2,1)S(1)} %copy.8), channel_id=1, source_target_pairs={{0,1},{1,2},{2,3},{3,4},{4,5},{5,6},{6,7},{8,9},{9,10},{10,11},{11... | collective-permute-start | bytes 202760 | tf_op jit(solution)/shard_map/ppermute | solution.py:308
  368.2 5.2 copy-start.1
  408.7 1.4 copy-start.7
  408.7 2.0 copy-start.8
  410.7 9.5 %copy-start.6 = (bf16[2,1024,512]{2,1,0:T(8,128)(2,1)}, bf16[2,1024,512]{2,1,0:T(8,128)(2,1)S(1)}, u32[]{:S(2)}) copy-start(bf16[2,1024,512]{2,1,0:T(8,128)(2,1)S(1)} %fusion) | copy-start | bytes 6291460
  410.7 5.2 collective-permute-start.4
  414.4 5.8 collective-permute-start.5
  420.9 151.2 %collective-permute-start.7 = (bf16[2,1056,16]{1,2,0:T(8,128)(2,1)S(1)}, bf16[2,1056,16]{1,2,0:T(8,128)(2,1)S(1)}, u32[]{:S(2)}, u32[]{:S(2)}) collective-permute-start(bf16[2,1056,16]{1,2,0:T(8,128)(2,1)S(1)} %copy.13), channel_id=1, source_target_pairs={{1,0},{2,1},{3,2},{4,3},{5,4},{6,5},{7,6},{9,8},{10,9},{11,10},{12... | collective-permute-start | bytes 202760 | tf_op jit(solution)/shard_map/ppermute | solution.py:310
  422.2 149.6 %collective-permute-start.6 = (bf16[2,1056,16]{1,2,0:T(8,128)(2,1)S(1)}, bf16[2,1056,16]{1,2,0:T(8,128)(2,1)S(1)}, u32[]{:S(2)}, u32[]{:S(2)}) collective-permute-start(bf16[2,1056,16]{1,2,0:T(8,128)(2,1)S(1)} %copy.12), channel_id=1, source_target_pairs={{0,1},{1,2},{2,3},{3,4},{4,5},{5,6},{6,7},{8,9},{9,10},{10,11},{11... | collective-permute-start | bytes 202760 | tf_op jit(solution)/shard_map/ppermute | solution.py:308
  577.4 29.4 %copy-start.2 = (f32[1024,512]{1,0:T(8,128)S(1)}, f32[1024,512]{1,0:T(8,128)}, u32[]{:S(2)}) copy-start(f32[1024,512]{1,0:T(8,128)} %param.7) | copy-start | bytes 6291460

commit v2 on v1

--- a/solution.py
+++ b/solution.py
@@ -8,6 +8,7 @@
 from jax.sharding import PartitionSpec as P
 
 OMAX = 16
+LANES = 128
 
 
 step_size = 0.25
@@ -27,13 +28,13 @@
 
 def commutator_kernel(first, nz, nc, *refs):
     if first:
-        (real, imag, ham, out_real, out_imag, ham_rows_out, ham_cols_out,
-         ham_rows, ham_cols, real_rows, imag_rows, real_cols, imag_cols,
-         xy_send, xy_recv, z_send, z_recv, local_sem) = refs
+        (real, imag, ham, out_real, out_imag, real_wide, imag_wide, ham_rows_out, ham_cols_out,
+         ham_rows, ham_cols, real_rows, imag_rows, real_cols, imag_cols, corners,
+         xy_send, xy_recv, z_send, z_recv, corner_send, corner_recv, local_sem) = refs
     else:
-        (real, imag, ham_rows_in, ham_cols_in, out_real, out_imag,
-         ham_rows, ham_cols, real_rows, imag_rows, real_cols, imag_cols,
-         xy_send, xy_recv, z_send, z_recv, local_sem) = refs
+        (real, imag, ham_rows_in, ham_cols_in, out_real, out_imag, real_wide, imag_wide,
+         ham_rows, ham_cols, real_rows, imag_rows, real_cols, imag_cols, corners,
+         xy_send, xy_recv, z_send, z_recv, corner_send, corner_recv, local_sem) = refs
         ham = None
     height, breadth = real.shape
     z = lax.axis_index("row")
@@ -77,7 +78,30 @@
         pl.semaphore_signal(barrier, inc=1, device_id=(neighbour, c), device_id_type=pl.DeviceIdType.MESH)
     for b in range(bits):
         pl.semaphore_signal(barrier, inc=1, device_id=(z, flip(c, b)), device_id_type=pl.DeviceIdType.MESH)
-    pl.semaphore_wait(barrier, 2 + bits)
+    left = lax.rem(c + nc - 1, nc)
+    right = lax.rem(c + 1, nc)
+    diagonals = [(v, h) for v in (0, 1) for h in (0, 1)]
+
+    def diagonal(v, h):
+        return ((up, down)[v], (right, left)[h])
+
+    for v, h in diagonals:
+        pl.semaphore_signal(barrier, inc=1, device_id=diagonal(v, h), device_id_type=pl.DeviceIdType.MESH)
+    pl.semaphore_wait(barrier, 2 + bits + 4)
+
+    def corner_copy(side, v, h):
+        own = (real, imag)[side]
+        rows = pl.ds(height - OMAX if v == 0 else 0, OMAX)
+        cols = pl.ds(breadth - LANES if h == 0 else 0, LANES)
+        slot = side * 4 + v * 2 + h
+        return pltpu.make_async_remote_copy(
+            src_ref=own.at[rows, cols],
+            dst_ref=corners.at[slot],
+            send_sem=corner_send.at[slot],
+            recv_sem=corner_recv.at[slot],
+            device_id=diagonal(v, h),
+            device_id_type=pl.DeviceIdType.MESH,
+        )
 
     def xy_copy(p, mask, t):
         own, panel, (start, size), order = pieces[p]
@@ -115,14 +139,19 @@
         copy.start()
         started.append(copy)
 
-    for p in range(len(pieces)):
-        for t in range(bits):
-            begin(xy_copy(p, 0, t))
-    for p in range(len(rings)):
-        plan = ring_plan(nz, rings[p][3])
-        for direction in (0, 1):
-            if plan[direction] >= 1:
-                begin(z_copy(p, direction, 1))
+    def begin_own(which):
+        for p in which:
+            for t in range(bits):
+                begin(xy_copy(p, 0, t))
+            plan = ring_plan(nz, rings[p][3])
+            for direction in (0, 1):
+                if plan[direction] >= 1:
+                    begin(z_copy(p, direction, 1))
+
+    for side in (0, 1):
+        for v, h in diagonals:
+            begin(corner_copy(side, v, h))
+    begin_own((0, 1))
 
     if first:
         locals_in = [
@@ -165,6 +194,8 @@
                 for p in (0, 1):
                     for event in ring_events(p, mask):
                         advance_z(*event)
+            if mask == 1:
+                begin_own((2, 3))
         for step in range(nc, ring_steps + 1):
             for p in (0, 1):
                 for event in ring_events(p, step):
@@ -244,6 +275,23 @@
         while done_steps < want:
             done_steps += 1
             consume_ring(done_steps)
+    for side, (rows, cols, wide) in enumerate(((real_rows, real_cols, real_wide), (imag_rows, imag_cols, imag_wide))):
+        own = (real, imag)[side]
+        for v, h in diagonals:
+            corner_copy(side, v, h).wait_recv()
+        middle = pl.ds(OMAX, height)
+        inner = pl.ds(LANES, breadth)
+        above, below = pl.ds(0, OMAX), pl.ds(OMAX + height, OMAX)
+        before, after = pl.ds(0, LANES), pl.ds(LANES + breadth, LANES)
+        wide[middle, inner] = own[...]
+        wide[above, inner] = cols[down, pl.ds(height - OMAX, OMAX), :]
+        wide[below, inner] = cols[up, pl.ds(0, OMAX), :]
+        wide[middle, before] = rows[left, :, pl.ds(breadth - LANES, LANES)]
+        wide[middle, after] = rows[right, :, pl.ds(0, LANES)]
+        wide[above, before] = corners[side * 4]
+        wide[above, after] = corners[side * 4 + 1]
+        wide[below, before] = corners[side * 4 + 2]
+        wide[below, after] = corners[side * 4 + 3]
     for copy in started:
         copy.wait_send()
     for copy in outs:
@@ -259,8 +307,9 @@
     low = jnp.bfloat16
     rows_shape = (nc, height, breadth)
     cols_shape = (nz, height, breadth)
-    out_shape = [drift_shape, drift_shape]
-    out_specs = [vmem, vmem]
+    wide_shape = jax.ShapeDtypeStruct((height + 2 * OMAX, breadth + 2 * LANES), low)
+    out_shape = [drift_shape, drift_shape, wide_shape, wide_shape]
+    out_specs = [vmem] * 4
     if first:
         out_shape += [jax.ShapeDtypeStruct(rows_shape, low), jax.ShapeDtypeStruct(cols_shape, low)]
         out_specs += [anywhere, anywhere]
@@ -283,10 +332,13 @@
             pltpu.VMEM(rows_shape, low),
             pltpu.VMEM(cols_shape, low),
             pltpu.VMEM(cols_shape, low),
+            pltpu.VMEM((8, OMAX, LANES), low),
             pltpu.SemaphoreType.DMA((count, nc)),
             pltpu.SemaphoreType.DMA((count, nc)),
             pltpu.SemaphoreType.DMA((count, 2, nz)),
             pltpu.SemaphoreType.DMA((count, 2, nz)),
+            pltpu.SemaphoreType.DMA((8,)),
+            pltpu.SemaphoreType.DMA((8,)),
             pltpu.SemaphoreType.DMA((2,)),
         ],
         compiler_params=pltpu.CompilerParams(
@@ -297,54 +349,100 @@
     )(*operands)
 
 
-def extended(cells, sides, width):
-    for axis, dim in sides:
-        count = lax.axis_size(axis)
-        ends = count - 1
-        head = lax.slice_in_dim(cells, 0, width, axis=dim)
-        tail = lax.slice_in_dim(cells, cells.shape[dim] - width, cells.shape[dim], axis=dim)
-        cells = jnp.concatenate(
-            [
-                lax.ppermute(tail, axis, [(i, (i + 1) % count) for i in range(ends)]),
-                cells,
-                lax.ppermute(head, axis, [((i + 1) % count, i) for i in range(ends)]),
-            ],
-            axis=dim,
-        )
-    return cells
-
-
-def dissipate(matrix, padded, amplitudes, offsets, active, row_first, col_first):
-    height = matrix.shape[1]
-    breadth = matrix.shape[2]
-    levels = amplitudes.shape[1]
-    margin = (padded.shape[1] - height) // 2
-    positions = jnp.arange(levels, dtype=jnp.int32)
-    summed = jnp.zeros(matrix.shape, matrix.dtype)
-    for jump_slot in range(amplitudes.shape[0]):
-        offset = offsets[jump_slot]
-        inside = (positions + offset >= 0) & (positions + offset < levels)
-        strength = jnp.where(inside, amplitudes[jump_slot], 0.0)
-        outflow = jnp.pad(strength * strength, (margin, margin))
-        outflow = lax.dynamic_slice_in_dim(outflow, margin - offset, levels)
-        row_strength = lax.dynamic_slice_in_dim(strength, row_first, height)
-        col_strength = lax.dynamic_slice_in_dim(strength, col_first, breadth)
-        row_outflow = lax.dynamic_slice_in_dim(outflow, row_first, height)
-        col_outflow = lax.dynamic_slice_in_dim(outflow, col_first, breadth)
-        corner = margin + offset
-        shifted = lax.dynamic_slice(padded, (jnp.int32(0), corner, corner), (2, height, breadth))
-        contribution = (
-            row_strength[:, None] * col_strength[None, :] * shifted
-            - 0.5 * (row_outflow[:, None] + col_outflow[None, :]) * matrix
-        )
-        summed = summed + jnp.where(jump_slot < active, contribution, 0.0)
-    return summed
-
-
 def diagonal_sum(matrix, row_first, col_first):
     row_index = lax.broadcasted_iota(jnp.int32, matrix.shape, 0) + row_first
     col_index = lax.broadcasted_iota(jnp.int32, matrix.shape, 1) + col_first
     return jnp.sum(jnp.where(row_index == col_index, matrix, 0.0))
+
+
+def dissipate_kernel(last, slots, offsets, scale, *refs):
+    if last:
+        (real, imag, first_real, first_imag, turn_real, turn_imag, real_wide, imag_wide,
+         row_rate, col_rate, out_real, out_imag, real_full, imag_full) = refs
+    else:
+        (real, imag, turn_real, turn_imag, real_wide, imag_wide,
+         row_rate, col_rate, out_real, out_imag, low_real, low_imag, real_full, imag_full) = refs
+    step = pl.program_id(0)
+    tile, breadth = real.shape
+    width = real_full.shape[1]
+    factor = scale[0]
+
+    @pl.when(step == 0)
+    def _():
+        rows = pl.ds(0, real_wide.shape[0])
+        real_full[rows, :] = real_wide[...].astype(jnp.float32)
+        imag_full[rows, :] = imag_wide[...].astype(jnp.float32)
+
+    sums = [jnp.zeros((tile, breadth), jnp.float32) for _ in range(2)]
+    for slot in range(slots):
+        offset = offsets[slot]
+        whole_rows = (OMAX + offset) // 8
+        spare_rows = OMAX + offset - whole_rows * 8
+        weight = row_rate[:, slot : slot + 1] * col_rate[slot : slot + 1, :]
+        for side, full in enumerate((real_full, imag_full)):
+            strip = full[pl.ds(pl.multiple_of(step * tile + whole_rows * 8, 8), tile + 8), :]
+            strip = pltpu.roll(strip, width - LANES - offset, 1)[:, :breadth]
+            strip = pltpu.roll(strip, lax.rem(tile + 8 - spare_rows, tile + 8), 0)[:tile, :]
+            sums[side] += weight * strip
+    loss = -0.5 * (row_rate[:, slots : slots + 1] + col_rate[slots : slots + 1, :])
+    if last:
+        sides = ((real, first_real, turn_real, out_real), (imag, first_imag, turn_imag, out_imag))
+        for side, (start, first, turn, out) in enumerate(sides):
+            middle = (start[...] + step_size * first[...]) * factor
+            second = turn[...] + sums[side] + loss * middle
+            out[...] = (start[...] + 0.5 * step_size * (first[...] + second)) * factor
+    else:
+        sides = ((real, turn_real, out_real, low_real), (imag, turn_imag, out_imag, low_imag))
+        for side, (start, turn, out, low) in enumerate(sides):
+            first = turn[...] + sums[side] + loss * start[...]
+            out[...] = first
+            low[...] = ((start[...] + step_size * first) * factor).astype(jnp.bfloat16)
+
+
+def finish_drift(last, offsets, scale, tiled, wides, row_rate, col_rate):
+    height, breadth = tiled[0].shape
+    slots = offsets.shape[0]
+    tile = min(128, height)
+    smem = pl.BlockSpec(memory_space=pltpu.SMEM)
+    block = pl.BlockSpec((tile, breadth), lambda i: (i, 0))
+
+    def whole(array):
+        return pl.BlockSpec(array.shape, lambda i: (0, 0))
+
+    shape = jax.ShapeDtypeStruct((height, breadth), jnp.float32)
+    low_shape = jax.ShapeDtypeStruct((height, breadth), jnp.bfloat16)
+    out_shape = [shape, shape] if last else [shape, shape, low_shape, low_shape]
+    return pl.pallas_call(
+        functools.partial(dissipate_kernel, last, slots),
+        grid=(height // tile,),
+        out_shape=out_shape,
+        in_specs=[smem, smem]
+        + [block] * len(tiled)
+        + [whole(wide) for wide in wides]
+        + [pl.BlockSpec((tile, row_rate.shape[1]), lambda i: (i, 0)), whole(col_rate)],
+        out_specs=[block] * len(out_shape),
+        scratch_shapes=[pltpu.VMEM((wides[0].shape[0] + 8, wides[0].shape[1]), jnp.float32)] * 2,
+        compiler_params=pltpu.CompilerParams(
+            dimension_semantics=("arbitrary",), vmem_limit_bytes=40 * 1024 * 1024
+        ),
+        cost_estimate=pl.CostEstimate(
+            flops=60 * height * breadth, bytes_accessed=40 * height * breadth, transcendentals=0
+        ),
+        name="last_dissipator" if last else "first_dissipator",
+    )(offsets, scale, *tiled, *wides, row_rate, col_rate)
+
+
+def rates(amplitudes, offsets, active):
+    slots, levels = amplitudes.shape
+    positions = jnp.arange(levels, dtype=jnp.int32)
+    target = positions[None, :] + offsets[:, None]
+    inside = (target >= 0) & (target < levels) & (jnp.arange(slots)[:, None] < active)
+    strength = jnp.where(inside, amplitudes, 0.0)
+    squares = jnp.pad(strength * strength, ((0, 0), (OMAX, OMAX)))
+    outflow = jnp.zeros((levels,), jnp.float32)
+    for slot in range(slots):
+        outflow = outflow + lax.dynamic_slice(squares, (slot, OMAX - offsets[slot]), (1, levels))[0]
+    return jnp.concatenate([strength, outflow[None, :], jnp.zeros((7, levels), jnp.float32)], axis=0)
 
 
 def local(nz, nc, rho_real, rho_imag, hamiltonian, amplitudes, offsets, active_jumps):
@@ -352,28 +450,31 @@
     levels = amplitudes.shape[1]
     row_first = lax.axis_index("row") * height
     col_first = lax.axis_index("col") * breadth
-    active = active_jumps[0]
-    start_trace = lax.psum(diagonal_sum(rho_real, row_first, col_first), ("row", "col"))
-
-    def drift(real_part, imag_part, panels):
-        real_low = real_part.astype(jnp.bfloat16)
-        imag_low = imag_part.astype(jnp.bfloat16)
-        real_turn, imag_turn, *made = commutator(real_low, imag_low, hamiltonian, panels, nz, nc)
-        matrix = jnp.stack([real_part, imag_part])
-        padded = extended(matrix.astype(jnp.bfloat16), (("row", 1), ("col", 2)), OMAX).astype(
-            matrix.dtype
+    partial = diagonal_sum(rho_real, row_first, col_first)
+    partials = lax.all_gather(jnp.full((8, LANES), partial), ("row", "col"), axis=0, tiled=False)
+    scale = (levels / jnp.sum(partials[:, 0, 0])).reshape(1)
+    table = rates(amplitudes, offsets, active_jumps[0])
+    row_rate = lax.dynamic_slice_in_dim(table, row_first, height, axis=1).T
+    col_rate = lax.dynamic_slice_in_dim(table, col_first, breadth, axis=1)
+
+    turn_real, turn_imag, real_wide, imag_wide, *panels = commutator(
+        rho_real.astype(jnp.bfloat16), rho_imag.astype(jnp.bfloat16), hamiltonian, None, nz, nc
+    )
+    first_real, first_imag, low_real, low_imag = finish_drift(
+        False, offsets, scale, (rho_real, rho_imag, turn_real, turn_imag), (real_wide, imag_wide), row_rate, col_rate
+    )
+    turn_real, turn_imag, real_wide, imag_wide = commutator(low_real, low_imag, hamiltonian, panels, nz, nc)
+    return tuple(
+        finish_drift(
+            True,
+            offsets,
+            scale,
+            (rho_real, rho_imag, first_real, first_imag, turn_real, turn_imag),
+            (real_wide, imag_wide),
+            row_rate,
+            col_rate,
         )
-        loss = dissipate(matrix, padded, amplitudes, offsets, active, row_first, col_first)
-        return real_turn + loss[0], imag_turn + loss[1], made
-
-    first_real, first_imag, panels = drift(rho_real, rho_imag, None)
-    rescale = levels / start_trace
-    middle_real = (rho_real + step_size * first_real) * rescale
-    middle_imag = (rho_imag + step_size * first_imag) * rescale
-    second_real, second_imag, _ = drift(middle_real, middle_imag, panels)
-    updated_real = rho_real + 0.5 * step_size * (first_real + second_real)
-    updated_imag = rho_imag + 0.5 * step_size * (first_imag + second_imag)
-    return (updated_real * rescale, updated_imag * rescale)
+    )
 
 
 def solution(mesh):

time: 619 us -> 512 us (0.83)
  other arithmetic: 117 us -> 7.87 us
  Pallas kernels: 401 us -> 425 us
  starting transfers between devices: 20.1 us -> 0 us
  local copies, waits for them, and re-layouts: 7.63 us -> 24.1 us
  between operations: 27.4 us -> 12.3 us
    pallas_call x0 -> x2, Pallas kernels: none -> 59.3 us  [finish_drift(): pl.pallas_call(functools.partial(dissipate_kernel, last, slots), grid=(he...]
    add x2 -> x1, other arithmetic: 57.7 us -> 0.37 us  [rates(): outflow + lax.dynamic_slice(squares, (slot, OMAX - offsets[slot]), (1, le...]
    unnamed x0 -> x1, blocking collectives: none -> 41.9 us
    psum x1 -> x0, blocking collectives: 40.3 us -> none  [local(): lax.psum(diagonal_sum(rho_real, row_first, col_first), ('row', 'col'))]
    pallas_call x2, Pallas kernels: 401 us -> 366 us  [commutator(): pl.pallas_call(functools.partial(commutator_kernel, first, nz, nc), out_s...]
    mul x17 -> x1, other arithmetic: 35.2 us -> 1.02 us  [rates(): squares = jnp.pad(strength * strength, ((0, 0), (OMAX, OMAX)))]
    ppermute x8 -> x0, starting transfers between devices: 20.1 us -> none  [the longest x4 14.9 us: extended(): lax.ppermute(tail, axis, [(i, (i + 1) % count) for i in range(ends)])]
    unnamed x22 -> x36, local copies, waits for them, and re-layouts: 2.97 us -> 22.2 us
  transfers between devices with their start and end apart: 8 -> 0, of which waited for: 2 -> 0; matrix products, arithmetic and copies ran while one was open for 5% -> 0% of each run, Pallas kernels for 65% -> 0%
where the time goes in v2:
time: 512 us; the launch traced here: 511 us
  Pallas kernels  425 us (83%)
  blocking collectives  41.9 us (8%)
  local copies, waits for them, and re-layouts  24.1 us (5%)
  between operations  12.3 us (2%)
  other arithmetic  7.87 us (2%)
    pallas_call x2, Pallas kernels, commutator(): pl.pallas_call(functools.partial(commutator_kernel, first, nz, nc), out_s...  366 us
    pallas_call x2, Pallas kernels, finish_drift(): pl.pallas_call(functools.partial(dissipate_kernel, last, slots), grid=(he...  59.3 us
    unnamed x1, blocking collectives  41.9 us
    unnamed x36, local copies, waits for them, and re-layouts  22.2 us

profile of v2, /device:TPU:0, one launch (start us, length us, event | category | flops | bytes accessed | tf_op | source)
XLA Modules:
  0.0 511.3 jit_solution(1272874864136930347)
XLA Ops:
  1.4 1.6 fusion.15
  13.3 1.0 fusion.12
  15.0 4.7 fusion.14
  20.4 41.9 %all-reduce.1 = f32[32]{0:T(128)S(1)} all-reduce(f32[32]{0:T(128)S(1)} %dynamic-update-slice), channel_id=2, replica_groups=mesh['row'=4,'col'=8] {'row','col'}, use_global_device_ids=true, to_apply=%add.1 | all-reduce | flops 32 | bytes 256
  63.7 1.1 convert_element_type.9.refs_1_
  64.8 217.5 %first_commutator.1 = (f32[1024,512]{1,0:T(8,128)}, f32[1024,512]{1,0:T(8,128)}, bf16[1056,768]{1,0:T(8,128)(2,1)}, bf16[1056,768]{1,0:T(8,128)(2,1)}, bf16[8,10...) custom-call(bf16[1024,512]{1,0:T(8,128)(2,1)} %get-tuple-element.32.refs_0_, ...), custom_call_target="tpu_custom_call" | custom-call | flops 17179869184 | bytes 8388608 | tf_op jit(solution)/shard_map/first_commutator/pallas_call | solution.py:323
  282.3 1.6 copy-done
  283.9 1.6 copy-done.3
  285.5 1.4 copy-done.10
  286.9 1.4 copy-done.11
  288.3 29.0 %first_dissipator.1 = (f32[1024,512]{1,0:T(8,128)S(1)}, f32[1024,512]{1,0:T(8,128)S(1)}, bf16[1024,512]{1,0:T(8,128)(2,1)S(1)}, bf16[1024,512]{1,0:T(8,128)(2,1)S(1)}) custom-call(s32[8]{0:T(128)S(1)} %copy-done.14, f32[1]{0:T(128)} %bitcast.1.scale, f32[1024,512]{1,0:T(8,128)S(1)} %copy-done, f32[1024,512]{1,0:T(8,128)S(1)} %copy-done.3, ...), custom_call_target="tpu_custom_call" | custom-call | flops 31457280 | bytes 20971520 | tf_op jit(solution)/shard_map/first_dissipator/pallas_call | solution.py:415
  317.3 1.3 copy-done.5
  318.6 1.3 copy-done.7
  320.0 1.0 copy-done.15
  321.0 1.0 copy-done.16
  321.9 148.3 %second_commutator.1 = (f32[1024,512]{1,0:T(8,128)}, f32[1024,512]{1,0:T(8,128)}, bf16[1056,768]{1,0:T(8,128)(2,1)}, bf16[1056,768]{1,0:T(8,128)(2,1)}) custom-call(bf16[1024,512]{1,0:T(8,128)(2,1)} %copy-done.15, bf16[1024,512]{1,0:T(8,128)(2,1)} %copy-done.16, bf16[8,1024,512]{2,1,0:T(8,128)(2,1)} %get-tuple-element.24.refs_2_, ...), custom_call_target="tpu_custom_call" | custom-call | flops 17179869184 | bytes 8388608 | tf_op jit(solution)/shard_map/second_commutator/pallas_call | solution.py:323
  470.2 1.6 copy-done.1
  471.8 1.6 copy-done.4
  473.4 1.6 copy-done.6
  475.0 1.6 copy-done.8
  476.6 1.6 copy-done.9
  478.2 1.4 copy-done.12
  479.6 1.4 copy-done.13
  481.0 30.3 %last_dissipator.1 = (f32[1024,512]{1,0:T(8,128)}, f32[1024,512]{1,0:T(8,128)}) custom-call(s32[8]{0:T(128)S(1)} %copy-done.14, f32[1]{0:T(128)} %bitcast.1.scale, f32[1024,512]{1,0:T(8,128)S(1)} %copy-done.1, f32[1024,512]{1,0:T(8,128)S(1)} %copy-done.4, f32[1024,512]{1,0:T(8,128)S(1)} %copy-done.6, f32[1024,512]{1,0:T(8,128)S(1)} %copy-done.8, ...), custom_call_target="tpu_custom_call" | custom-call | flops 31457280 | bytes 20971520 | tf_op jit(solution)/shard_map/last_dissipator/pallas_call | solution.py:415
  (32 shorter events, 2.2 us)
Async XLA Ops:
  14.7 49.0 %copy-start.2 = (f32[1024,512]{1,0:T(8,128)S(1)}, f32[1024,512]{1,0:T(8,128)}, u32[]{:S(2)}) copy-start(f32[1024,512]{1,0:T(8,128)} %refs_1_.3) | copy-start | bytes 6291460
  64.8 217.5 %copy-start.14 = (s32[8]{0:T(128)S(1)}, s32[8]{0:T(128)}, u32[]{:S(2)}) copy-start(s32[8]{0:T(128)} %offsets.3) | copy-start | bytes 100
  282.3 1.6 copy-start
  283.9 1.6 copy-start.3
  285.5 1.4 copy-start.10
  286.9 1.4 copy-start.11
  317.3 1.3 copy-start.5
  318.6 1.3 copy-start.7
  320.0 1.0 copy-start.15
  321.0 1.0 copy-start.16
  470.2 1.6 copy-start.1
  471.8 1.6 copy-start.4
  473.4 1.6 copy-start.6
  475.0 1.6 copy-start.8
  476.6 1.6 copy-start.9
  478.2 1.4 copy-start.12
  479.6 1.4 copy-start.13

commit v3 on v2

--- a/solution.py
+++ b/solution.py
@@ -423,7 +423,7 @@
         out_specs=[block] * len(out_shape),
         scratch_shapes=[pltpu.VMEM((wides[0].shape[0] + 8, wides[0].shape[1]), jnp.float32)] * 2,
         compiler_params=pltpu.CompilerParams(
-            dimension_semantics=("arbitrary",), vmem_limit_bytes=40 * 1024 * 1024
+            dimension_semantics=("arbitrary",), vmem_limit_bytes=VMEM_LIMIT
         ),
         cost_estimate=pl.CostEstimate(
             flops=60 * height * breadth, bytes_accessed=40 * height * breadth, transcendentals=0
@@ -451,8 +451,8 @@
     row_first = lax.axis_index("row") * height
     col_first = lax.axis_index("col") * breadth
     partial = diagonal_sum(rho_real, row_first, col_first)
-    partials = lax.all_gather(jnp.full((8, LANES), partial), ("row", "col"), axis=0, tiled=False)
-    scale = (levels / jnp.sum(partials[:, 0, 0])).reshape(1)
+    start_trace = lax.psum(lax.psum(partial, "row"), "col")
+    scale = (levels / start_trace).reshape(1)
     table = rates(amplitudes, offsets, active_jumps[0])
     row_rate = lax.dynamic_slice_in_dim(table, row_first, height, axis=1).T
     col_rate = lax.dynamic_slice_in_dim(table, col_first, breadth, axis=1)

time: 512 us -> 476 us (0.930)
  local copies, waits for them, and re-layouts: 24.1 us -> 3.31 us
  blocking collectives: 41.9 us -> 26.5 us
    unnamed x1 -> x0, blocking collectives: 41.9 us -> none
    psum x0 -> x2, blocking collectives: none -> 26.5 us  [local(): start_trace = lax.psum(lax.psum(partial, 'row'), 'col')]
    unnamed x36 -> x2, local copies, waits for them, and re-layouts: 22.2 us -> 0.01 us
where the time goes in v3:
time: 476 us
  Pallas kernels  427 us (90%)
  blocking collectives  26.5 us (6%)
  between operations  12.2 us (3%)
  other arithmetic  7.09 us (1%)
    pallas_call x2, Pallas kernels, commutator(): pl.pallas_call(functools.partial(commutator_kernel, first, nz, nc), out_s...  363 us
    pallas_call x2, Pallas kernels, finish_drift(): pl.pallas_call(functools.partial(dissipate_kernel, last, slots), grid=(he...  63.3 us
    psum x2, blocking collectives, local(): start_trace = lax.psum(lax.psum(partial, 'row'), 'col')  26.5 us

profile of v3, /device:TPU:0, one launch (start us, length us, event | category | flops | bytes accessed | tf_op | source)
XLA Modules:
  0.0 475.7 jit_solution(6100596162440874383)
XLA Ops:
  1.3 0.1 pad.7.clone
  1.4 1.6 fusion.15
  13.1 1.0 fusion.12
  14.1 0.4 fusion.11
  14.5 0.0 copy-start
  14.5 0.1 maximum_maximum_fusion
  14.6 0.6 constant_dynamic-slice_fusion.refs_7_.refs_9_
  15.2 1.0 copy.8.refs_6_.refs_8_
  16.2 4.5 fusion.14
  20.7 14.1 %psum.14 = f32[]{:T(128)} all-reduce(f32[]{:T(128)} %get-tuple-element.33), channel_id=1, replica_groups=mesh['row'=4,'col'=8] {'row'}, use_global_device_ids=true, to_apply=%region_1.2 | all-reduce | flops 1 | bytes 8 | tf_op jit(solution)/shard_map/psum | solution.py:454
  34.8 12.4 %psum.15 = f32[]{:T(128)} all-reduce(f32[]{:T(128)} %psum.14), channel_id=1, replica_groups=mesh['row'=4,'col'=8] {'col'}, use_global_device_ids=true, to_apply=%region_2.3 | all-reduce | flops 1 | bytes 8 | tf_op jit(solution)/shard_map/psum | solution.py:454
  47.9 0.0 copy-done
  47.9 1.1 convert_element_type.9.refs_1_
  49.0 216.3 %first_commutator.1 = (f32[1024,512]{1,0:T(8,128)}, f32[1024,512]{1,0:T(8,128)}, bf16[1056,768]{1,0:T(8,128)(2,1)}, bf16[1056,768]{1,0:T(8,128)(2,1)}, bf16[8,10...) custom-call(bf16[1024,512]{1,0:T(8,128)(2,1)} %get-tuple-element.32.refs_0_, ...), custom_call_target="tpu_custom_call" | custom-call | flops 17179869184 | bytes 8388608 | tf_op jit(solution)/shard_map/first_commutator/pallas_call | solution.py:323
  265.3 31.3 %first_dissipator.1 = (f32[1024,512]{1,0:T(8,128)}, f32[1024,512]{1,0:T(8,128)}, bf16[1024,512]{1,0:T(8,128)(2,1)}, bf16[1024,512]{1,0:T(8,128)(2,1)}) custom-call(s32[8]{0:T(128)} %offsets.3, f32[1]{0:T(128)} %bitcast.scale, f32[1024,512]{1,0:T(8,128)} %refs_0_.3, f32[1024,512]{1,0:T(8,128)} %refs_1_.3, f32[1024,512]{1,0:T(8,128)} %get-tuple-element.16.refs_2_, ...), custom_call_target="tpu_custom_call" | custom-call | flops 31457280 | bytes 20971520 | tf_op jit(solution)/shard_map/first_dissipator/pallas_call | solution.py:415
  296.6 146.9 %second_commutator.1 = (f32[1024,512]{1,0:T(8,128)}, f32[1024,512]{1,0:T(8,128)}, bf16[1056,768]{1,0:T(8,128)(2,1)}, bf16[1056,768]{1,0:T(8,128)(2,1)}) custom-call(bf16[1024,512]{1,0:T(8,128)(2,1)} %get-tuple-element.22.refs_0_, bf16[1024,512]{1,0:T(8,128)(2,1)} %get-tuple-element.23.refs_1_, bf16[8,1024,512]{2,1,0:T(8,128)(2,1)} %get-tuple-element.24.refs_2_, ...), custom_call_target="tpu_custom_call" | custom-call | flops 17179869184 | bytes 8388608 | tf_op jit(solution)/shard_map/second_commutator/pallas_call | solution.py:323
  443.5 32.0 %last_dissipator.1 = (f32[1024,512]{1,0:T(8,128)}, f32[1024,512]{1,0:T(8,128)}) custom-call(s32[8]{0:T(128)} %offsets.3, f32[1]{0:T(128)} %bitcast.scale, f32[1024,512]{1,0:T(8,128)} %refs_0_.3, f32[1024,512]{1,0:T(8,128)} %refs_1_.3, f32[1024,512]{1,0:T(8,128)} %get-tuple-element.20.refs_2_, f32[1024,512]{1,0:T(8,128)} %get-tuple-element.21.refs_3_, ...), custom_call_target="tpu_custom_call" | custom-call | flops 31457280 | bytes 20971520 | tf_op jit(solution)/shard_map/last_dissipator/pallas_call | solution.py:415
  (5 shorter events, 0.0 us)
Async XLA Ops:
  14.5 33.4 %copy-start = (f32[1024,512]{1,0:T(8,128)S(1)}, f32[1024,512]{1,0:T(8,128)}, u32[]{:S(2)}) copy-start(f32[1024,512]{1,0:T(8,128)} %refs_1_.3) | copy-start | bytes 6291460
